TPU v7x, 32 devices: a whole 2x2x4 slice. The times are simulated.
32 devices in a mesh: ep: 16 (over z, y, x), dp: 2 (over core).
Axes of the slice: x: 2, y: 2, z: 4, core: 2. Of those that a mesh axis runs over, the one named last changes fastest.
Arguments:
- grad_out: bfloat16 [4096, 2048], P(('ep', 'dp')), may hold values from -6 to 6
- router_prob: bfloat16 [4096], P(('ep', 'dp')), may hold values from 0.19921875 to 1
- routes: int32 [4096, 1], P(('ep', 'dp')), may hold values from 0 to 63, as said below
- token_inputs: bfloat16 [4096, 2048], P(('ep', 'dp')), may hold values from -6 to 6
- w_in: bfloat16 [7168, 2048], P(('ep', 'dp')), may hold values from -0.125 to 0.125
- w_out: bfloat16 [7168, 2048], P(('ep', 'dp')), may hold values from -0.0625 to 0.0625
Outputs:
- grad_tokens: bfloat16 [4096, 2048], P(('ep', 'dp'))
- grad_in_weight: bfloat16 [7168, 2048], P(('ep', 'dp'))
- grad_out_weight: bfloat16 [7168, 2048], P(('ep', 'dp'))
Inputs may be any that keep to these rules, and one draw needn't show every extreme that they name: `routes`: ids below 1 are the experts of this window; the rows of one device name each of them at most 3 times, and in every draw one of them is named exactly 3 times by the rows of every device of one dp index.
All inputs are finite; a program needn't handle non-finite values.
Results may differ from a plain program's by a relative error of at most 0.014.
Values may be sent and summed in bfloat16 or wider, within the bound.
A program may use at most 64 MiB of HBM per device.

v0:
```python
import math

import jax
import jax.numpy as jnp
from jax import lax
from jax.sharding import PartitionSpec as P

GROUP = 16
CAP = 3


def per_device(grad_out, router_prob, routes, token_inputs, w_in, w_out):
    ep_count = lax.axis_size("ep")
    replicas = lax.axis_size("dp")
    flight = ep_count // GROUP
    tok_rows = grad_out.shape[0]
    model_width = grad_out.shape[1]
    expert_ids = routes[:, 0]
    in_window = expert_ids < flight
    onehot = (expert_ids[:, None] == jnp.arange(flight, dtype=jnp.int32)[None, :]).astype(
        jnp.bfloat16
    )
    earlier = (
        jnp.arange(tok_rows, dtype=jnp.int32)[:, None]
        > jnp.arange(tok_rows, dtype=jnp.int32)[None, :]
    ).astype(jnp.bfloat16)
    before = jnp.dot(earlier, onehot, preferred_element_type=jnp.float32)
    slot_rank = jnp.sum(before * onehot.astype(jnp.float32), axis=1).astype(jnp.int32)
    window_rows = flight * CAP
    target = jnp.where(in_window, expert_ids * CAP + slot_rank, window_rows)
    chooser = (jnp.arange(window_rows, dtype=jnp.int32)[:, None] == target[None, :]).astype(
        jnp.bfloat16
    )
    scaled = (router_prob.astype(jnp.float32)[:, None] * grad_out.astype(jnp.float32)).astype(
        jnp.bfloat16
    )
    paired = jnp.concatenate((scaled, token_inputs), axis=1)
    outgoing = jnp.dot(chooser, paired, preferred_element_type=jnp.float32).astype(jnp.bfloat16)
    outgoing = jnp.broadcast_to(
        outgoing.reshape(flight, 1, CAP, 2 * model_width), (flight, GROUP, CAP, 2 * model_width)
    )
    outgoing = outgoing.reshape(ep_count, CAP, 2 * model_width)
    incoming = lax.all_to_all(outgoing, "ep", split_axis=0, concat_axis=0, tiled=True)
    slot_total = ep_count * CAP
    incoming = incoming.reshape(slot_total, 2 * model_width)
    cotangent = incoming[:, :model_width]
    rows_in = incoming[:, model_width:]
    weight_in, weight_out = (
        lax.all_gather(w_in, "dp", axis=0, tiled=True),
        lax.all_gather(w_out, "dp", axis=0, tiled=True),
    )
    contract_last = (((1,), (1,)), ((), ()))
    contract_first = (((0,), (0,)), ((), ()))
    pre_act = lax.dot_general(rows_in, weight_in, contract_last, preferred_element_type=jnp.float32)
    gate_sig = jax.nn.sigmoid(pre_act)
    hidden = (pre_act * gate_sig).astype(jnp.bfloat16)
    back_prop = lax.dot_general(
        cotangent, weight_out, contract_last, preferred_element_type=jnp.float32
    )
    grad_pre = (back_prop * gate_sig * (1.0 + pre_act * (1.0 - gate_sig))).astype(jnp.bfloat16)
    piece_grad = jnp.dot(grad_pre, weight_in, preferred_element_type=jnp.float32).astype(
        jnp.bfloat16
    )
    piece_grad = piece_grad.reshape(ep_count, CAP, model_width)
    returned = lax.all_to_all(piece_grad, "ep", split_axis=0, concat_axis=0, tiled=True)
    summed = jnp.sum(returned.reshape(flight, GROUP, CAP, model_width).astype(jnp.float32), axis=1)
    summed = summed.reshape(window_rows, model_width)
    picked = jnp.take(summed, jnp.minimum(target, window_rows - 1), axis=0)
    grad_tokens = jnp.where(in_window[:, None], picked, jnp.float32(0.0)).astype(jnp.bfloat16)
    grad_scale = 1.0 / math.sqrt(replicas * slot_total)
    columns = grad_pre
    grad_in = lax.psum_scatter(
        lax.dot_general(
            columns, rows_in, contract_first, preferred_element_type=jnp.float32
        ).astype(jnp.bfloat16),
        "dp",
        scatter_dimension=0,
        tiled=True,
    ).astype(jnp.float32)
    columns = hidden
    grad_outw = lax.psum_scatter(
        lax.dot_general(
            columns, cotangent, contract_first, preferred_element_type=jnp.float32
        ).astype(jnp.bfloat16),
        "dp",
        scatter_dimension=0,
        tiled=True,
    ).astype(jnp.float32)
    return (
        grad_tokens,
        (grad_in * grad_scale).astype(jnp.bfloat16),
        (grad_outw * grad_scale).astype(jnp.bfloat16),
    )


def solution(mesh):
    in_specs = (
        P(("ep", "dp"), None),
        P(("ep", "dp")),
        P(("ep", "dp"), None),
        P(("ep", "dp"), None),
        P(("ep", "dp"), None),
        P(("ep", "dp"), None),
    )
    out_specs = (P(("ep", "dp"), None), P(("ep", "dp"), None), P(("ep", "dp"), None))
    return jax.shard_map(
        per_device, mesh=mesh, in_specs=in_specs, out_specs=out_specs, check_vma=False
    )
```

profile of v0, /device:TPU:0, one launch (start us, length us, event | category | flops | bytes accessed | tf_op | source)
XLA Modules:
  0.0 73.3 jit_solution(5831370888514954435)
XLA Ops:
  7.2 0.0 copy-start.4
  7.2 0.0 copy-start.2
  7.2 0.0 copy-start.1
  7.2 0.0 copy-start.3
  7.2 0.0 all-gather.5.cloned.1.call-start
  7.2 0.7 all-gather.5.cloned.1.call-update
  7.9 0.0 all-gather.3.cloned.1.call-start
  8.0 0.7 all-gather.3.cloned.1.call-update
  8.7 0.0 reduce-scatter.3.cloned.1.call-start
  8.7 0.0 copy-done.4
  8.8 0.0 copy-done.2
  8.8 0.1 fusion.5
  8.9 0.0 copy-done.1
  8.9 0.2 multiply_convert_fusion.2
  9.1 0.0 copy-done.3
  9.1 0.3 convolution_convert_fusion
  9.3 0.2 reshape.59
  9.6 23.2 %all_to_all.10 = bf16[16,3,4096]{2,1,0:T(4,128)(2,1)S(1)} all-to-all(bf16[16,3,4096]{2,1,0:T(4,128)(2,1)S(1)} %reshape.59), channel_id=1, replica_groups=mesh['ep'=16,'dp'=2] {'ep'}, dimensions={0} | all-to-all | bytes 786432 | tf_op jit(solution)/shard_map/all_to_all | solution.py:43
  32.8 0.3 reshape.60
  33.1 0.0 all-gather.5.cloned.1.call-done
  33.1 2.4 %fusion.10 = f32[48,448]{1,0:T(8,128)S(1)} fusion(bf16[448,2048]{1,0:T(8,128)(2,1)} %all-gather.5.cloned.1.call-done, bf16[48,4096]{1,0:T(8,128)(2,1)S(1)} %reshape.60), kind=kOutput, calls=%fused_computation.22 | convolution fusion | flops 88080384 | bytes 2117632 | tf_op jit(solution)/shard_map/dot_general | solution.py:54
  35.5 0.0 all-gather.3.cloned.1.call-done
  35.6 2.1 %fusion.1 = bf16[48,448]{1,0:T(8,128)(2,1)S(1)} fusion(bf16[448,2048]{1,0:T(8,128)(2,1)} %all-gather.3.cloned.1.call-done, bf16[48,4096]{1,0:T(8,128)(2,1)S(1)} %reshape.60, f32[48,448]{1,0:T(8,128)S(1)} %fusion.10), kind=kOutput, calls=%fused_computation.9 | convolution fusion | flops 88273920 | bytes 2172928 | tf_op jit(solution)/shard_map/dot_general | solution.py:57
  37.7 1.9 %convolution_convert_fusion.2 = bf16[448,2048]{1,0:T(8,128)(2,1)} fusion(bf16[48,448]{1,0:T(8,128)(2,1)S(1)} %fusion.1, bf16[48,4096]{1,0:T(8,128)(2,1)S(1)} %reshape.60), kind=kOutput, calls=%fused_computation.3 | convolution fusion | flops 88997888 | bytes 2080768 | tf_op jit(solution)/shard_map/dot_general | solution.py:73
  39.6 0.0 reduce-scatter.3.cloned.1.call-update
  39.6 0.0 copy-start
  39.6 0.0 reduce-scatter.5.cloned.1.call-start
  39.7 1.9 %convolution_convert_fusion.1 = bf16[448,2048]{1,0:T(8,128)(2,1)} fusion(bf16[48,4096]{1,0:T(8,128)(2,1)S(1)} %reshape.60, f32[48,448]{1,0:T(8,128)S(1)} %fusion.10), kind=kOutput, calls=%fused_computation.2 | convolution fusion | flops 89105408 | bytes 2129920 | tf_op jit(solution)/shard_map/dot_general | solution.py:82
  41.6 0.0 reduce-scatter.5.cloned.1.call-update
  41.6 0.0 copy-done
  41.7 0.4 convolution_convert_fusion.3
  42.1 0.8 %reshape.61 = bf16[16,3,2048]{2,1,0:T(4,128)(2,1)} reshape(bf16[48,2048]{1,0:T(8,128)(2,1)S(1)} %convolution_convert_fusion.3) | data formatting | bytes 393216 | tf_op jit(solution)/shard_map/reshape | solution.py:64
  42.9 6.7 %all-to-all-start.1 = ((bf16[16,3,2048]{2,1,0:T(4,128)(2,1)}), bf16[16,3,2048]{2,1,0:T(4,128)(2,1)S(1)}, u32[]{:S(2)}, u32[]{:S(2)}) async-start(bf16[16,3,2048]{2,1,0:T(4,128)(2,1)} %reshape.61), calls=%async_computation.1 | async-start | bytes 524288 | tf_op jit(solution)/shard_map/all_to_all | solution.py:65
  49.7 10.3 %all-to-all-done.1 = bf16[16,3,2048]{2,1,0:T(4,128)(2,1)S(1)} async-done(((bf16[16,3,2048]{2,1,0:T(4,128)(2,1)}), bf16[16,3,2048]{2,1,0:T(4,128)(2,1)S(1)}, u32[]{:S(2)}, u32[]{:S(2)}) %all-to-all-start.1) | async-done | bytes 196640 | tf_op jit(solution)/shard_map/all_to_all | solution.py:65
  59.9 0.1 convert_reduce_fusion
  60.1 0.9 %gather_fusion = bf16[128,2048]{1,0:T(8,128)(2,1)S(1)} fusion(bf16[3,2048]{1,0:T(4,128)(2,1)S(1)} %convert_reduce_fusion, s32[1024]{0:T(1024)S(1)} %pad_clamp_fusion), kind=kCustom, calls=%fused_computation | custom fusion | bytes 1049088 | tf_op jit(solution)/shard_map/jit(_take)/gather | solution.py:68
  61.0 1.1 %select_convert_fusion = bf16[128,2048]{1,0:T(8,128)(2,1)} fusion(bf16[128,2048]{1,0:T(8,128)(2,1)S(1)} %gather_fusion, pred[128]{0:T(512)(128)(4,1)S(1)} %get-tuple-element.3, pred[128]{0:T(512)(128)(4,1)S(1)} %get-tuple-element.4), kind=kLoop, calls=%fused_computation.18 | loop fusion | flops 524288 | bytes 1048832 | tf_op jit(solution)/shard_map/convert_element_type | solution.py:69
  62.1 0.0 reduce-scatter.3.cloned.1.call-done
  62.1 2.3 %multiply_convert_fusion.1 = bf16[224,2048]{1,0:T(8,128)(2,1)} fusion(bf16[224,2048]{1,0:T(8,128)(2,1)} %reduce-scatter.3.cloned.1.call-done), kind=kLoop, calls=%fused_computation.6 | loop fusion | flops 1376256 | bytes 1835008 | tf_op jit(solution)/shard_map/convert_element_type | solution.py:91
  64.4 0.0 reduce-scatter.5.cloned.1.call-done
  64.4 2.3 %multiply_convert_fusion = bf16[224,2048]{1,0:T(8,128)(2,1)} fusion(bf16[224,2048]{1,0:T(8,128)(2,1)} %reduce-scatter.5.cloned.1.call-done), kind=kLoop, calls=%fused_computation.5 | loop fusion | flops 1376256 | bytes 1835008 | tf_op jit(solution)/shard_map/convert_element_type | solution.py:92
  (4 shorter events, 0.0 us)
Async XLA Ops:
  7.2 1.6 %copy-start.4 = (bf16[128]{0:T(256)(128)(2,1)S(1)}, bf16[128]{0:T(256)(128)(2,1)}, u32[]{:S(2)}) copy-start(bf16[128]{0:T(256)(128)(2,1)} %param.7) | copy-start | bytes 772
  7.2 1.6 %copy-start.2 = (s32[128,1]{0,1:T(1,128)S(1)}, s32[128,1]{0,1:T(1,128)}, u32[]{:S(2)}) copy-start(s32[128,1]{0,1:T(1,128)} %param.8) | copy-start | bytes 1540
  7.2 1.7 %copy-start.1 = (bf16[128,2048]{1,0:T(8,128)(2,1)S(1)}, bf16[128,2048]{1,0:T(8,128)(2,1)}, u32[]{:S(2)}) copy-start(bf16[128,2048]{1,0:T(8,128)(2,1)} %param.6) | copy-start | bytes 1572868
  7.2 1.9 %copy-start.3 = (bf16[128,2048]{1,0:T(8,128)(2,1)S(1)}, bf16[128,2048]{1,0:T(8,128)(2,1)}, u32[]{:S(2)}) copy-start(bf16[128,2048]{1,0:T(8,128)(2,1)} %param.9) | copy-start | bytes 1572868
  7.2 25.9 %all-gather.5.cloned.1.call-start = ((), (), s32[]{:S(2)}) async-start(), calls=%async_computation.5 | async-start | bytes 2752512 | tf_op jit(solution)/shard_map/all_gather | solution.py:49
  7.9 27.6 %all-gather.3.cloned.1.call-start = ((), (), s32[]{:S(2)}) async-start(), calls=%async_computation.4 | async-start | bytes 2752512 | tf_op jit(solution)/shard_map/all_gather | solution.py:50
  8.7 53.4 %reduce-scatter.3.cloned.1.call-start = ((), (), s32[]{:S(2)}) async-start(), calls=%async_computation.6 | async-start | bytes 2752512 | tf_op jit(solution)/shard_map/reduce_scatter | solution.py:72
  39.6 2.0 %copy-start = (bf16[448,2048]{1,0:T(8,128)(2,1)S(1)}, bf16[448,2048]{1,0:T(8,128)(2,1)}, u32[]{:S(2)}) copy-start(bf16[448,2048]{1,0:T(8,128)(2,1)} %all-gather.5.cloned.1.call-done) | copy-start | bytes 5505028
  39.6 24.8 %reduce-scatter.5.cloned.1.call-start = ((), (), s32[]{:S(2)}) async-start(), calls=%async_computation.7 | async-start | bytes 2752512 | tf_op jit(solution)/shard_map/reduce_scatter | solution.py:81
  42.9 17.0 %all-to-all-start.1 = ((bf16[16,3,2048]{2,1,0:T(4,128)(2,1)}), bf16[16,3,2048]{2,1,0:T(4,128)(2,1)S(1)}, u32[]{:S(2)}, u32[]{:S(2)}) async-start(bf16[16,3,2048]{2,1,0:T(4,128)(2,1)} %reshape.61), calls=%async_computation.1 | async-start | bytes 524288 | tf_op jit(solution)/shard_map/all_to_all | solution.py:65
Sparse Core Ops, SparseCore 0:
  9.6 12.8 all-gather.4
  24.0 11.3 all-gather.2
  39.7 10.4 reduce-scatter.2
  52.3 10.6 reduce-scatter.4
where the time goes:
time: 73.7 us; the launch traced here: 73.3 us
  blocking collectives  23.2 us (31%)
  between operations  13.9 us (19%)
  waiting for transfers between devices  11.7 us (16%)
  matrix products  9.18 us (12%)
  starting transfers between devices  6.83 us (9%)
  other arithmetic  6.04 us (8%)
  local copies, waits for them, and re-layouts  2.31 us (3%)
    all_to_all x1, blocking collectives, per_device(): lax.all_to_all(outgoing, 'ep', split_axis=0, concat_axis=0, tiled=True)  23.2 us
    all_to_all x1, waiting for transfers between devices, per_device(): lax.all_to_all(piece_grad, 'ep', split_axis=0, concat_axis=0, tiled=True)  10.3 us
    all_to_all x1, starting transfers between devices, per_device(): lax.all_to_all(piece_grad, 'ep', split_axis=0, concat_axis=0, tiled=True)  6.67 us
    dot_general x1, matrix products, per_device(): lax.dot_general(rows_in, weight_in, contract_last, preferred_element_type...  2.38 us
    convert_element_type x1, other arithmetic, per_device(): (grad_in * grad_scale).astype(jnp.bfloat16)  2.35 us
    convert_element_type x1, other arithmetic, per_device(): (grad_outw * grad_scale).astype(jnp.bfloat16)  2.28 us
    dot_general x1, matrix products, per_device(): lax.dot_general(cotangent, weight_out, contract_last, preferred_element_t...  2.12 us
    dot_general x1, matrix products, per_device(): lax.dot_general(columns, cotangent, contract_first, preferred_element_typ...  1.95 us
  transfers between devices with their start and end apart: 5, of which 1 were waited for; matrix products, arithmetic and copies ran while one was open for 15% of the time, Pallas kernels for 0%

commit v1 on v0

--- a/solution.py
+++ b/solution.py
@@ -1,12 +1,18 @@
+import functools
 import math
 
 import jax
 import jax.numpy as jnp
 from jax import lax
+from jax.experimental import pallas as pl
+from jax.experimental.pallas import tpu as pltpu
 from jax.sharding import PartitionSpec as P
 
 GROUP = 16
 CAP = 3
+LINES = 8
+LANES = 128
+MESH = pl.DeviceIdType.MESH
 
 
 def per_device(grad_out, router_prob, routes, token_inputs, w_in, w_out):
@@ -93,6 +99,281 @@
     )
 
 
+def fused_kernel(
+    n,
+    inner,
+    grad_out,
+    prob,
+    routes,
+    tokens,
+    w_in,
+    w_out,
+    tok_out,
+    gin_out,
+    gout_out,
+    go_v,
+    ti_v,
+    wi_v,
+    wo_v,
+    recv,
+    x32,
+    q_b,
+    x_b,
+    hid_v,
+    gp_v,
+    ret32,
+    ret_send,
+    ret_recv,
+    d_send,
+    d_recv,
+    g_v,
+    tok_v,
+    load_sem,
+    w_send,
+    w_recv,
+    a_send,
+    a_recv,
+    r_send,
+    r_recv,
+    d_ssem,
+    d_rsem,
+    out_sem,
+):
+    me = lax.axis_index("ep")
+    core = lax.axis_index("dp")
+    partner = 1 - core
+    outer = n // inner
+    o, i = me // inner, me % inner
+    rows, width = w_in.shape
+    tok_rows = tokens.shape[0]
+    block_rows = CAP * LINES
+    half = LINES // 2
+    wide = 2 * width // LINES
+    narrow = width // LINES
+    slots = n * CAP
+    f32, bf16 = jnp.float32, jnp.bfloat16
+
+    def to(src, dst, send, arrive, ep, dp):
+        return pltpu.make_async_remote_copy(
+            src_ref=src,
+            dst_ref=dst,
+            send_sem=send,
+            recv_sem=arrive,
+            device_id=(ep, dp),
+            device_id_type=MESH,
+        )
+
+    barrier = pltpu.get_barrier_semaphore()
+    for k in range(1, n):
+        pl.semaphore_signal(barrier, inc=1, device_id=((me + k) % n, core), device_id_type=MESH)
+    pl.semaphore_signal(barrier, inc=1, device_id=(me, partner), device_id_type=MESH)
+
+    load_go = pltpu.make_async_copy(grad_out, go_v, load_sem.at[0])
+    load_ti = pltpu.make_async_copy(tokens, ti_v, load_sem.at[1])
+    mine = pl.ds(pl.multiple_of(core * rows, rows), rows)
+    theirs = pl.ds(pl.multiple_of(partner * rows, rows), rows)
+    load_wi = pltpu.make_async_copy(w_in, wi_v.at[mine], load_sem.at[2])
+    load_wo = pltpu.make_async_copy(w_out, wo_v.at[mine], load_sem.at[3])
+    load_go.start()
+    load_ti.start()
+    load_wi.start()
+    load_wo.start()
+
+    line = lax.broadcasted_iota(jnp.int32, (block_rows, tok_rows), 0)
+    in_window = jnp.broadcast_to((routes[...] < 1).astype(f32), (block_rows, tok_rows))
+    earlier = (
+        lax.broadcasted_iota(jnp.int32, (tok_rows, tok_rows), 0)
+        < lax.broadcasted_iota(jnp.int32, (tok_rows, tok_rows), 1)
+    ).astype(f32).astype(bf16)
+    rank = jnp.dot(in_window.astype(bf16), earlier, preferred_element_type=f32)
+    rank_of_line = (line // LINES).astype(f32)
+    sel = jnp.where(rank == rank_of_line, in_window, 0.0)
+    weight = jnp.sum(sel * prob[...].astype(f32), axis=1, keepdims=True)
+    lane_of = line % LINES
+    weight = jnp.where(lane_of[:, :1] < half, weight, 1.0)
+    load_go.wait()
+    load_ti.wait()
+    block = jnp.zeros((block_rows, wide), f32)
+    for g in range(LINES):
+        picked = jnp.where(lane_of == g, sel, 0.0).astype(bf16)
+        source = go_v if g < half else ti_v
+        columns = pl.ds((g % half) * wide, wide)
+        block += jnp.dot(picked, source[:, columns], preferred_element_type=f32)
+    recv[me] = (block * weight).astype(bf16)
+    pl.semaphore_wait(barrier, n)
+
+    sends = []
+
+    def spread(b, ep):
+        copy = to(recv.at[b], recv.at[b], a_send.at[len(sends)], a_recv.at[b], ep, core)
+        copy.start()
+        sends.append(copy)
+
+    def arrived(b):
+        to(recv.at[b], recv.at[b], a_send.at[0], a_recv.at[b], me, partner).wait_recv()
+
+    def unpack(b):
+        at = pl.ds(pl.multiple_of(b * block_rows, LINES), block_rows)
+        for c in range(wide // LANES):
+            x32[c, at, :] = recv[b, :, pl.ds(c * LANES, LANES)].astype(f32)
+
+    for k in range(outer - 1, 0, -1):
+        spread(me, ((o + k) % outer) * inner + i)
+    for j in range(1, inner):
+        spread(me, o * inner + (i + j) % inner)
+    push_wi = to(w_in, wi_v.at[mine], w_send.at[0], w_recv.at[0], me, partner)
+    push_wo = to(w_out, wo_v.at[mine], w_send.at[1], w_recv.at[1], me, partner)
+    push_wi.start()
+    push_wo.start()
+    unpack(me)
+    for k in range(1, outer):
+        b = ((o + outer - k) % outer) * inner + i
+        arrived(b)
+        for j in range(1, inner):
+            spread(b, o * inner + (i + j) % inner)
+        unpack(b)
+    load_wi.wait()
+    load_wo.wait()
+    to(w_in, wi_v.at[theirs], w_send.at[0], w_recv.at[0], me, partner).wait_recv()
+    to(w_out, wo_v.at[theirs], w_send.at[1], w_recv.at[1], me, partner).wait_recv()
+    for k in range(outer):
+        for j in range(1, inner):
+            b = ((o + outer - k) % outer) * inner + (i + inner - j) % inner
+            arrived(b)
+            unpack(b)
+
+    for g in range(LINES):
+        dest = q_b if g < half else x_b
+        for c in range(wide // LANES):
+            columns = pl.ds((g % half) * wide + c * LANES, LANES)
+            dest[:, columns] = x32[c, pl.ds(g, slots, stride=LINES), :].astype(bf16)
+
+    last = (((1,), (1,)), ((), ()))
+    pre = lax.dot_general(wi_v[...], x_b[...], last, preferred_element_type=f32)
+    back = lax.dot_general(wo_v[...], q_b[...], last, preferred_element_type=f32)
+    sig = jax.nn.sigmoid(pre)
+    grad_pre = back * sig * (1.0 + pre * (1.0 - sig))
+    gp_v[...] = grad_pre.astype(bf16)
+    hid_v[...] = (pre * sig).astype(bf16)
+    flat = grad_pre.T.astype(bf16)
+    for g in range(LINES):
+        piece = jnp.dot(flat, wi_v[:, pl.ds(g * narrow, narrow)], preferred_element_type=f32)
+        for c in range(narrow // LANES):
+            ret32[c, pl.ds(g, slots, stride=LINES), :] = piece[:, c * LANES : (c + 1) * LANES]
+    for b in range(n):
+        for c in range(narrow // LANES):
+            ret_send[b, :, pl.ds(c * LANES, LANES)] = ret32[
+                c, pl.ds(b * block_rows, block_rows), :
+            ].astype(bf16)
+    returns = []
+    for k in range(n - 1, 0, -1):
+        dst = (me + k) % n
+        copy = to(ret_send.at[dst], ret_recv.at[me], r_send.at[k - 1], r_recv.at[me], dst, core)
+        copy.start()
+        returns.append(copy)
+
+    chunk = 512
+    swaps = []
+    for w, (left, right) in enumerate(((gp_v, x_b), (hid_v, q_b))):
+        for c in range(0, width, chunk):
+            cols = pl.ds(c, chunk)
+            d_send[w, :, cols] = jnp.dot(
+                left[theirs, :], right[:, cols], preferred_element_type=f32
+            ).astype(bf16)
+        copy = to(d_send.at[w], d_recv.at[w], d_ssem.at[w], d_rsem.at[w], me, partner)
+        copy.start()
+        swaps.append(copy)
+    grad_scale = 1.0 / math.sqrt(2 * slots)
+    outs = []
+    for w, (left, right, out) in enumerate(((gp_v, x_b, gin_out), (hid_v, q_b, gout_out))):
+        swaps[w].wait_recv()
+        for c in range(0, width, chunk):
+            cols = pl.ds(c, chunk)
+            own = jnp.dot(left[mine, :], right[:, cols], preferred_element_type=f32)
+            total = own.astype(bf16).astype(f32) + d_recv[w, :, cols].astype(f32)
+            g_v[w, :, cols] = (total * grad_scale).astype(bf16)
+        copy = pltpu.make_async_copy(g_v.at[w], out, out_sem.at[w])
+        copy.start()
+        outs.append(copy)
+
+    summed = ret_send[me].astype(f32)
+    for k in range(1, n):
+        b = (me + n - k) % n
+        to(ret_send.at[b], ret_recv.at[b], r_send.at[0], r_recv.at[b], me, partner).wait_recv()
+        summed += ret_recv[b].astype(f32)
+    rounded = summed.astype(bf16)
+    for g in range(LINES):
+        picked = jnp.where(lane_of == g, sel, 0.0).T.astype(bf16)
+        tok_v[:, pl.ds(g * narrow, narrow)] = jnp.dot(
+            picked, rounded, preferred_element_type=f32
+        ).astype(bf16)
+    copy = pltpu.make_async_copy(tok_v, tok_out, out_sem.at[2])
+    copy.start()
+    outs.append(copy)
+    for copy in sends + returns + swaps + [push_wi, push_wo]:
+        copy.wait_send()
+    for copy in outs:
+        copy.wait()
+
+
+def per_device_fused(grad_out, router_prob, routes, token_inputs, w_in, w_out):
+    n = lax.axis_size("ep")
+    inner = 1 << (n.bit_length() // 2)
+    tok_rows, width = token_inputs.shape
+    rows = w_in.shape[0]
+    block_rows = CAP * LINES
+    wide = 2 * width // LINES
+    narrow = width // LINES
+    slots = n * CAP
+    f32, bf16 = jnp.float32, jnp.bfloat16
+    copies = n - 1
+    dma = pltpu.SemaphoreType.DMA
+    anywhere = pl.BlockSpec(memory_space=pl.ANY)
+    vmem = pl.BlockSpec(memory_space=pltpu.VMEM)
+    return pl.pallas_call(
+        functools.partial(fused_kernel, n, inner),
+        out_shape=(
+            jax.ShapeDtypeStruct((tok_rows, width), bf16),
+            jax.ShapeDtypeStruct((rows, width), bf16),
+            jax.ShapeDtypeStruct((rows, width), bf16),
+        ),
+        in_specs=[anywhere, vmem, vmem, anywhere, anywhere, anywhere],
+        out_specs=(anywhere, anywhere, anywhere),
+        scratch_shapes=[
+            pltpu.VMEM((tok_rows, width), bf16),
+            pltpu.VMEM((tok_rows, width), bf16),
+            pltpu.VMEM((2 * rows, width), bf16),
+            pltpu.VMEM((2 * rows, width), bf16),
+            pltpu.VMEM((n, block_rows, wide), bf16),
+            pltpu.VMEM((wide // LANES, n * block_rows, LANES), f32),
+            pltpu.VMEM((slots, width), bf16),
+            pltpu.VMEM((slots, width), bf16),
+            pltpu.VMEM((2 * rows, slots), bf16),
+            pltpu.VMEM((2 * rows, slots), bf16),
+            pltpu.VMEM((narrow // LANES, n * block_rows, LANES), f32),
+            pltpu.VMEM((n, block_rows, narrow), bf16),
+            pltpu.VMEM((n, block_rows, narrow), bf16),
+            pltpu.VMEM((2, rows, width), bf16),
+            pltpu.VMEM((2, rows, width), bf16),
+            pltpu.VMEM((2, rows, width), bf16),
+            pltpu.VMEM((tok_rows, width), bf16),
+            dma((4,)),
+            dma((2,)),
+            dma((2,)),
+            dma((copies,)),
+            dma((n,)),
+            dma((copies,)),
+            dma((n,)),
+            dma((2,)),
+            dma((2,)),
+            dma((3,)),
+        ],
+        compiler_params=pltpu.CompilerParams(
+            collective_id=0, has_side_effects=True, vmem_limit_bytes=40 * 1024 * 1024
+        ),
+    )(grad_out, router_prob.reshape(1, tok_rows), routes.reshape(1, tok_rows), token_inputs, w_in, w_out)
+
+
 def solution(mesh):
     in_specs = (
         P(("ep", "dp"), None),
@@ -103,6 +384,7 @@
         P(("ep", "dp"), None),
     )
     out_specs = (P(("ep", "dp"), None), P(("ep", "dp"), None), P(("ep", "dp"), None))
+    fused = mesh.shape["ep"] == GROUP and mesh.shape["dp"] == 2
     return jax.shard_map(
-        per_device, mesh=mesh, in_specs=in_specs, out_specs=out_specs, check_vma=False
-    )
+        per_device_fused if fused else per_device, mesh=mesh, in_specs=in_specs, out_specs=out_specs, check_vma=False
+    )

time: 73.7 us -> 32.1 us (0.44)
  Pallas kernels: 0 us -> 23.4 us
  blocking collectives: 23.2 us -> 0 us
  between operations: 13.9 us -> 0.66 us
  waiting for transfers between devices: 11.7 us -> 0 us
  matrix products: 9.18 us -> 0 us
  starting transfers between devices: 6.83 us -> 0 us
  other arithmetic: 6.04 us -> 0 us
  local copies, waits for them, and re-layouts: 2.31 us -> 7.73 us
    pallas_call x0 -> x1, Pallas kernels: none -> 23.4 us  [per_device_fused(): pl.pallas_call(functools.partial(fused_kernel, n, inner), out_shape=(jax....]
    all_to_all x1 -> x0, blocking collectives: 23.2 us -> none  [per_device(): lax.all_to_all(outgoing, 'ep', split_axis=0, concat_axis=0, tiled=True)]
    all_to_all x1 -> x0, waiting for transfers between devices: 10.3 us -> none  [per_device(): lax.all_to_all(piece_grad, 'ep', split_axis=0, concat_axis=0, tiled=True)]
    dot_general x7 -> x0, matrix products: 9.18 us -> none  [the longest x1 2.38 us: per_device(): lax.dot_general(rows_in, weight_in, contract_last, preferred_element_type...]
    unnamed x10 -> x15, local copies, waits for them, and re-layouts: 0.02 us -> 7.73 us
    all_to_all x1 -> x0, starting transfers between devices: 6.67 us -> none  [per_device(): lax.all_to_all(piece_grad, 'ep', split_axis=0, concat_axis=0, tiled=True)]
    convert_element_type x5 -> x0, other arithmetic: 5.9 us -> none  [the longest x1 2.35 us: per_device(): (grad_in * grad_scale).astype(jnp.bfloat16)]
    unnamed x4 -> x0, waiting for transfers between devices: 1.41 us -> none
  transfers between devices with their start and end apart: 5 -> 0, of which waited for: 1 -> 0; matrix products, arithmetic and copies ran while one was open for 15% -> 0% of each run, Pallas kernels for 0% -> 0%
where the time goes in v1:
time: 32.1 us; the launch traced here: 31.8 us
  Pallas kernels  23.4 us (73%)
  local copies, waits for them, and re-layouts  7.73 us (24%)
  between operations  0.66 us (2%)
    pallas_call x1, Pallas kernels, per_device_fused(): pl.pallas_call(functools.partial(fused_kernel, n, inner), out_shape=(jax....  23.4 us
    unnamed x15, local copies, waits for them, and re-layouts  7.73 us

profile of v1, /device:TPU:0, one launch (start us, length us, event | category | flops | bytes accessed | tf_op | source)
XLA Modules:
  0.0 31.8 jit_solution(1114945990300468866)
XLA Ops:
  0.6 0.0 copy-start.4
  0.6 0.0 copy-start.5
  0.7 0.6 %copy-done.4 = bf16[128]{0:T(256)(128)(2,1)S(1)} copy-done((bf16[128]{0:T(256)(128)(2,1)S(1)}, bf16[128]{0:T(256)(128)(2,1)}, u32[]{:S(2)}) %copy-start.4) | copy-done | bytes 280
  1.3 0.0 copy-done.5
  1.3 0.0 copy-start
  1.3 1.2 %copy-done = bf16[224,2048]{1,0:T(8,128)(2,1)S(1)} copy-done((bf16[224,2048]{1,0:T(8,128)(2,1)S(1)}, bf16[224,2048]{1,0:T(8,128)(2,1)}, u32[]{:S(2)}) %copy-start) | copy-done | bytes 917528
  2.5 0.0 copy-start.1
  2.5 1.2 %copy-done.1 = bf16[224,2048]{1,0:T(8,128)(2,1)S(1)} copy-done((bf16[224,2048]{1,0:T(8,128)(2,1)S(1)}, bf16[224,2048]{1,0:T(8,128)(2,1)}, u32[]{:S(2)}) %copy-start.1) | copy-done | bytes 917528
  3.7 0.0 copy-start.2
  3.7 1.0 %copy-done.2 = bf16[128,2048]{1,0:T(8,128)(2,1)S(1)} copy-done((bf16[128,2048]{1,0:T(8,128)(2,1)S(1)}, bf16[128,2048]{1,0:T(8,128)(2,1)}, u32[]{:S(2)}) %copy-start.2) | copy-done | bytes 524312
  4.7 0.0 copy-start.3
  4.7 1.0 %copy-done.3 = bf16[128,2048]{1,0:T(8,128)(2,1)S(1)} copy-done((bf16[128,2048]{1,0:T(8,128)(2,1)S(1)}, bf16[128,2048]{1,0:T(8,128)(2,1)}, u32[]{:S(2)}) %copy-start.3) | copy-done | bytes 524312
  5.7 23.4 %shard_map.85 = (bf16[128,2048]{1,0:T(8,128)(2,1)S(1)}, bf16[224,2048]{1,0:T(8,128)(2,1)S(1)}, bf16[224,2048]{1,0:T(8,128)(2,1)S(1)}) custom-call(bf16[128,2048]{1,0:T(8,128)(2,1)S(1)} %copy-done.2, bf16[1,128]{1,0:T(2,128)(2,1)S(1)} %bitcast.2, s32[1,128]{1,0:T(1,128)S(1)} %bitcast.3, bf16[128,2048]{1,0:T(8,128)(2,1)S(1)} %copy-done.3, ...), custom_call_target="tpu_custom_call" | custom-call | tf_op jit(solution)/shard_map/pallas_call | solution.py:333
  29.1 0.8 %copy.12 = bf16[128,2048]{1,0:T(8,128)(2,1)} copy(bf16[128,2048]{1,0:T(8,128)(2,1)S(1)} %get-tuple-element.6) | data formatting | bytes 1048576
  29.9 0.9 %copy.13 = bf16[224,2048]{1,0:T(8,128)(2,1)} copy(bf16[224,2048]{1,0:T(8,128)(2,1)S(1)} %get-tuple-element.7) | data formatting | bytes 1835008
  30.9 0.9 %copy.14 = bf16[224,2048]{1,0:T(8,128)(2,1)} copy(bf16[224,2048]{1,0:T(8,128)(2,1)S(1)} %get-tuple-element.8) | data formatting | bytes 1835008
Async XLA Ops:
  0.6 0.7 %copy-start.4 = (bf16[128]{0:T(256)(128)(2,1)S(1)}, bf16[128]{0:T(256)(128)(2,1)}, u32[]{:S(2)}) copy-start(bf16[128]{0:T(256)(128)(2,1)} %param.7) | copy-start | bytes 772
  0.6 0.7 %copy-start.5 = (s32[128,1]{0,1:T(1,128)S(1)}, s32[128,1]{0,1:T(1,128)}, u32[]{:S(2)}) copy-start(s32[128,1]{0,1:T(1,128)} %param.8) | copy-start | bytes 1540
  1.3 1.2 %copy-start = (bf16[224,2048]{1,0:T(8,128)(2,1)S(1)}, bf16[224,2048]{1,0:T(8,128)(2,1)}, u32[]{:S(2)}) copy-start(bf16[224,2048]{1,0:T(8,128)(2,1)} %w_in.1) | copy-start | bytes 2752516
  2.5 1.2 %copy-start.1 = (bf16[224,2048]{1,0:T(8,128)(2,1)S(1)}, bf16[224,2048]{1,0:T(8,128)(2,1)}, u32[]{:S(2)}) copy-start(bf16[224,2048]{1,0:T(8,128)(2,1)} %w_out.1) | copy-start | bytes 2752516
  3.7 1.0 %copy-start.2 = (bf16[128,2048]{1,0:T(8,128)(2,1)S(1)}, bf16[128,2048]{1,0:T(8,128)(2,1)}, u32[]{:S(2)}) copy-start(bf16[128,2048]{1,0:T(8,128)(2,1)} %grad_out.1) | copy-start | bytes 1572868
  4.7 1.0 %copy-start.3 = (bf16[128,2048]{1,0:T(8,128)(2,1)S(1)}, bf16[128,2048]{1,0:T(8,128)(2,1)}, u32[]{:S(2)}) copy-start(bf16[128,2048]{1,0:T(8,128)(2,1)} %tokens.1) | copy-start | bytes 1572868

commit v2 on v1

--- a/solution.py
+++ b/solution.py
@@ -109,8 +109,7 @@
     w_in,
     w_out,
     tok_out,
-    gin_out,
-    gout_out,
+    grads_out,
     go_v,
     ti_v,
     wi_v,
@@ -126,8 +125,8 @@
     ret_recv,
     d_send,
     d_recv,
-    g_v,
-    tok_v,
+    prob_v,
+    routes_v,
     load_sem,
     w_send,
     w_recv,
@@ -137,7 +136,6 @@
     r_recv,
     d_ssem,
     d_rsem,
-    out_sem,
 ):
     me = lax.axis_index("ep")
     core = lax.axis_index("dp")
@@ -164,8 +162,12 @@
         )
 
     barrier = pltpu.get_barrier_semaphore()
-    for k in range(1, n):
-        pl.semaphore_signal(barrier, inc=1, device_id=((me + k) % n, core), device_id_type=MESH)
+    for k in range(1, outer):
+        peer = ((o + k) % outer) * inner + i
+        pl.semaphore_signal(barrier, inc=1, device_id=(peer, core), device_id_type=MESH)
+    for j in range(1, inner):
+        peer = o * inner + (i + j) % inner
+        pl.semaphore_signal(barrier, inc=1, device_id=(peer, core), device_id_type=MESH)
     pl.semaphore_signal(barrier, inc=1, device_id=(me, partner), device_id_type=MESH)
 
     load_go = pltpu.make_async_copy(grad_out, go_v, load_sem.at[0])
@@ -174,13 +176,19 @@
     theirs = pl.ds(pl.multiple_of(partner * rows, rows), rows)
     load_wi = pltpu.make_async_copy(w_in, wi_v.at[mine], load_sem.at[2])
     load_wo = pltpu.make_async_copy(w_out, wo_v.at[mine], load_sem.at[3])
+    load_prob = pltpu.make_async_copy(prob, prob_v, load_sem.at[4])
+    load_routes = pltpu.make_async_copy(routes, routes_v, load_sem.at[5])
+    load_routes.start()
+    load_prob.start()
     load_go.start()
     load_ti.start()
     load_wi.start()
     load_wo.start()
 
     line = lax.broadcasted_iota(jnp.int32, (block_rows, tok_rows), 0)
-    in_window = jnp.broadcast_to((routes[...] < 1).astype(f32), (block_rows, tok_rows))
+    load_routes.wait()
+    load_prob.wait()
+    in_window = jnp.broadcast_to((routes_v[...] < 1).astype(f32), (block_rows, tok_rows))
     earlier = (
         lax.broadcasted_iota(jnp.int32, (tok_rows, tok_rows), 0)
         < lax.broadcasted_iota(jnp.int32, (tok_rows, tok_rows), 1)
@@ -188,7 +196,7 @@
     rank = jnp.dot(in_window.astype(bf16), earlier, preferred_element_type=f32)
     rank_of_line = (line // LINES).astype(f32)
     sel = jnp.where(rank == rank_of_line, in_window, 0.0)
-    weight = jnp.sum(sel * prob[...].astype(f32), axis=1, keepdims=True)
+    weight = jnp.sum(sel * prob_v[...].astype(f32), axis=1, keepdims=True)
     lane_of = line % LINES
     weight = jnp.where(lane_of[:, :1] < half, weight, 1.0)
     load_go.wait()
@@ -200,7 +208,7 @@
         columns = pl.ds((g % half) * wide, wide)
         block += jnp.dot(picked, source[:, columns], preferred_element_type=f32)
     recv[me] = (block * weight).astype(bf16)
-    pl.semaphore_wait(barrier, n)
+    pl.semaphore_wait(barrier, outer + inner - 1)
 
     sends = []
 
@@ -284,17 +292,13 @@
         copy.start()
         swaps.append(copy)
     grad_scale = 1.0 / math.sqrt(2 * slots)
-    outs = []
-    for w, (left, right, out) in enumerate(((gp_v, x_b, gin_out), (hid_v, q_b, gout_out))):
+    for w, (left, right) in enumerate(((gp_v, x_b), (hid_v, q_b))):
         swaps[w].wait_recv()
         for c in range(0, width, chunk):
             cols = pl.ds(c, chunk)
             own = jnp.dot(left[mine, :], right[:, cols], preferred_element_type=f32)
             total = own.astype(bf16).astype(f32) + d_recv[w, :, cols].astype(f32)
-            g_v[w, :, cols] = (total * grad_scale).astype(bf16)
-        copy = pltpu.make_async_copy(g_v.at[w], out, out_sem.at[w])
-        copy.start()
-        outs.append(copy)
+            grads_out[w, :, cols] = (total * grad_scale).astype(bf16)
 
     summed = ret_send[me].astype(f32)
     for k in range(1, n):
@@ -304,15 +308,22 @@
     rounded = summed.astype(bf16)
     for g in range(LINES):
         picked = jnp.where(lane_of == g, sel, 0.0).T.astype(bf16)
-        tok_v[:, pl.ds(g * narrow, narrow)] = jnp.dot(
+        tok_out[:, pl.ds(g * narrow, narrow)] = jnp.dot(
             picked, rounded, preferred_element_type=f32
         ).astype(bf16)
-    copy = pltpu.make_async_copy(tok_v, tok_out, out_sem.at[2])
-    copy.start()
-    outs.append(copy)
     for copy in sends + returns + swaps + [push_wi, push_wo]:
         copy.wait_send()
-    for copy in outs:
+
+
+def write_kernel(tok_grad, grads, tok_out, gin_out, gout_out, sem):
+    copies = (
+        pltpu.make_async_copy(grads.at[0], gin_out, sem.at[0]),
+        pltpu.make_async_copy(grads.at[1], gout_out, sem.at[1]),
+        pltpu.make_async_copy(tok_grad, tok_out, sem.at[2]),
+    )
+    for copy in copies:
+        copy.start()
+    for copy in copies:
         copy.wait()
 
 
@@ -328,17 +339,16 @@
     f32, bf16 = jnp.float32, jnp.bfloat16
     copies = n - 1
     dma = pltpu.SemaphoreType.DMA
-    anywhere = pl.BlockSpec(memory_space=pl.ANY)
+    hbm = pl.BlockSpec(memory_space=pltpu.HBM)
     vmem = pl.BlockSpec(memory_space=pltpu.VMEM)
-    return pl.pallas_call(
+    tok_grad, grads = pl.pallas_call(
         functools.partial(fused_kernel, n, inner),
         out_shape=(
-            jax.ShapeDtypeStruct((tok_rows, width), bf16),
-            jax.ShapeDtypeStruct((rows, width), bf16),
-            jax.ShapeDtypeStruct((rows, width), bf16),
+            pltpu.VMEM((tok_rows, width), bf16),
+            pltpu.VMEM((2, rows, width), bf16),
         ),
-        in_specs=[anywhere, vmem, vmem, anywhere, anywhere, anywhere],
-        out_specs=(anywhere, anywhere, anywhere),
+        in_specs=[hbm] * 6,
+        out_specs=(vmem, vmem),
         scratch_shapes=[
             pltpu.VMEM((tok_rows, width), bf16),
             pltpu.VMEM((tok_rows, width), bf16),
@@ -355,9 +365,9 @@
             pltpu.VMEM((n, block_rows, narrow), bf16),
             pltpu.VMEM((2, rows, width), bf16),
             pltpu.VMEM((2, rows, width), bf16),
-            pltpu.VMEM((2, rows, width), bf16),
-            pltpu.VMEM((tok_rows, width), bf16),
-            dma((4,)),
+            pltpu.VMEM((1, tok_rows), bf16),
+            pltpu.VMEM((1, tok_rows), jnp.int32),
+            dma((6,)),
             dma((2,)),
             dma((2,)),
             dma((copies,)),
@@ -366,12 +376,23 @@
             dma((n,)),
             dma((2,)),
             dma((2,)),
-            dma((3,)),
         ],
         compiler_params=pltpu.CompilerParams(
-            collective_id=0, has_side_effects=True, vmem_limit_bytes=40 * 1024 * 1024
+            collective_id=0, has_side_effects=True, vmem_limit_bytes=63_000_000
         ),
     )(grad_out, router_prob.reshape(1, tok_rows), routes.reshape(1, tok_rows), token_inputs, w_in, w_out)
+    return pl.pallas_call(
+        write_kernel,
+        out_shape=(
+            jax.ShapeDtypeStruct((tok_rows, width), bf16),
+            jax.ShapeDtypeStruct((rows, width), bf16),
+            jax.ShapeDtypeStruct((rows, width), bf16),
+        ),
+        in_specs=[vmem, vmem],
+        out_specs=(hbm, hbm, hbm),
+        scratch_shapes=[dma((3,))],
+        compiler_params=pltpu.CompilerParams(vmem_limit_bytes=8 * 1024 * 1024),
+    )(tok_grad, grads)
 
 
 def solution(mesh):

time: 32.1 us -> 23.8 us (0.74)
  local copies, waits for them, and re-layouts: 7.73 us -> 0 us
    unnamed x15 -> x0, local copies, waits for them, and re-layouts: 7.73 us -> none
    pallas_call x1 -> x2, Pallas kernels: 23.4 us -> 23.1 us  [the longest x1 21.6 us: per_device_fused(): pl.pallas_call(functools.partial(fused_kernel, n, inner), out_shape=(pltp...]
where the time goes in v2:
time: 23.8 us; the launch traced here: 23.7 us
  Pallas kernels  23.1 us (97%)
  between operations  0.64 us (3%)
    pallas_call x1, Pallas kernels, per_device_fused(): pl.pallas_call(functools.partial(fused_kernel, n, inner), out_shape=(pltp...  21.6 us
    pallas_call x1, Pallas kernels, per_device_fused(): pl.pallas_call(write_kernel, out_shape=(jax.ShapeDtypeStruct((tok_rows, w...  1.43 us

profile of v2, /device:TPU:0, one launch (start us, length us, event | category | flops | bytes accessed | tf_op | source)
XLA Modules:
  0.0 23.7 jit_solution(6351962415907976538)
XLA Ops:
  0.6 21.6 %shard_map.85 = (bf16[128,2048]{1,0:T(8,128)(2,1)S(1)}, bf16[2,224,2048]{2,1,0:T(8,128)(2,1)S(1)}) custom-call(bf16[128,2048]{1,0:T(8,128)(2,1)} %grad_out.1, bf16[1,128]{1,0:T(2,128)(2,1)} %bitcast.2, s32[1,128]{1,0:T(1,128)} %bitcast.3, bf16[128,2048]{1,0:T(8,128)(2,1)} %tokens.1, bf16[224,2048]{1,0:T(8,128)(2,1)} %w_in.1, bf16[224,2048]{1,0:T(8,128)(2,1)} %w_out.1), custom_call_target="tpu_custom_call" | custom-call | tf_op jit(solution)/shard_map/pallas_call | solution.py:344
  22.3 1.4 %shard_map.86 = (bf16[128,2048]{1,0:T(8,128)(2,1)}, bf16[224,2048]{1,0:T(8,128)(2,1)}, bf16[224,2048]{1,0:T(8,128)(2,1)}) custom-call(bf16[128,2048]{1,0:T(8,128)(2,1)S(1)} %get-tuple-element.5.tok_grad, bf16[2,224,2048]{2,1,0:T(8,128)(2,1)S(1)} %get-tuple-element.6.grads), custom_call_target="tpu_custom_call" | custom-call | tf_op jit(solution)/shard_map/pallas_call | solution.py:384

commit v3 on v2

--- a/solution.py
+++ b/solution.py
@@ -274,7 +274,7 @@
                 c, pl.ds(b * block_rows, block_rows), :
             ].astype(bf16)
     returns = []
-    for k in range(n - 1, 0, -1):
+    for k in range(1, n):
         dst = (me + k) % n
         copy = to(ret_send.at[dst], ret_recv.at[me], r_send.at[k - 1], r_recv.at[me], dst, core)
         copy.start()

time: 23.8 us -> 23.5 us (0.987)
  the two profiles are of different devices: /device:TPU:0 before, /device:TPU:1 now
where the time goes in v3:
time: 23.5 us; the launch traced here: 23.3 us
  Pallas kernels  22.7 us (97%)
  between operations  0.64 us (3%)
    pallas_call x1, Pallas kernels, per_device_fused(): pl.pallas_call(functools.partial(fused_kernel, n, inner), out_shape=(pltp...  21.3 us
    pallas_call x1, Pallas kernels, per_device_fused(): pl.pallas_call(write_kernel, out_shape=(jax.ShapeDtypeStruct((tok_rows, w...  1.43 us

profile of v3, /device:TPU:1, one launch (start us, length us, event | category | flops | bytes accessed | tf_op | source)
XLA Modules:
  0.0 23.3 jit_solution(7189874853957662664)
XLA Ops:
  0.6 21.3 %shard_map.85 = (bf16[128,2048]{1,0:T(8,128)(2,1)S(1)}, bf16[2,224,2048]{2,1,0:T(8,128)(2,1)S(1)}) custom-call(bf16[128,2048]{1,0:T(8,128)(2,1)} %grad_out.1, bf16[1,128]{1,0:T(2,128)(2,1)} %bitcast.2, s32[1,128]{1,0:T(1,128)} %bitcast.3, bf16[128,2048]{1,0:T(8,128)(2,1)} %tokens.1, bf16[224,2048]{1,0:T(8,128)(2,1)} %w_in.1, bf16[224,2048]{1,0:T(8,128)(2,1)} %w_out.1), custom_call_target="tpu_custom_call" | custom-call | tf_op jit(solution)/shard_map/pallas_call | solution.py:344
  21.9 1.4 %shard_map.86 = (bf16[128,2048]{1,0:T(8,128)(2,1)}, bf16[224,2048]{1,0:T(8,128)(2,1)}, bf16[224,2048]{1,0:T(8,128)(2,1)}) custom-call(bf16[128,2048]{1,0:T(8,128)(2,1)S(1)} %get-tuple-element.5.tok_grad, bf16[2,224,2048]{2,1,0:T(8,128)(2,1)S(1)} %get-tuple-element.6.grads), custom_call_target="tpu_custom_call" | custom-call | tf_op jit(solution)/shard_map/pallas_call | solution.py:384

commit v4 on v3

--- a/solution.py
+++ b/solution.py
@@ -225,7 +225,7 @@
         for c in range(wide // LANES):
             x32[c, at, :] = recv[b, :, pl.ds(c * LANES, LANES)].astype(f32)
 
-    for k in range(outer - 1, 0, -1):
+    for k in range(1, outer):
         spread(me, ((o + k) % outer) * inner + i)
     for j in range(1, inner):
         spread(me, o * inner + (i + j) % inner)

time: 23.5 us -> 23 us (0.979)
  Pallas kernels: 22.7 us -> 22.2 us
    pallas_call x1, Pallas kernels: 21.3 us -> 20.8 us  [per_device_fused(): pl.pallas_call(functools.partial(fused_kernel, n, inner), out_shape=(pltp...]
where the time goes in v4:
time: 23 us; the launch traced here: 22.9 us
  Pallas kernels  22.2 us (97%)
  between operations  0.64 us (3%)
    pallas_call x1, Pallas kernels, per_device_fused(): pl.pallas_call(functools.partial(fused_kernel, n, inner), out_shape=(pltp...  20.8 us
    pallas_call x1, Pallas kernels, per_device_fused(): pl.pallas_call(write_kernel, out_shape=(jax.ShapeDtypeStruct((tok_rows, w...  1.43 us

profile of v4, /device:TPU:1, one launch (start us, length us, event | category | flops | bytes accessed | tf_op | source)
XLA Modules:
  0.0 22.9 jit_solution(14723662606830370738)
XLA Ops:
  0.6 20.8 %shard_map.85 = (bf16[128,2048]{1,0:T(8,128)(2,1)S(1)}, bf16[2,224,2048]{2,1,0:T(8,128)(2,1)S(1)}) custom-call(bf16[128,2048]{1,0:T(8,128)(2,1)} %grad_out.1, bf16[1,128]{1,0:T(2,128)(2,1)} %bitcast.2, s32[1,128]{1,0:T(1,128)} %bitcast.3, bf16[128,2048]{1,0:T(8,128)(2,1)} %tokens.1, bf16[224,2048]{1,0:T(8,128)(2,1)} %w_in.1, bf16[224,2048]{1,0:T(8,128)(2,1)} %w_out.1), custom_call_target="tpu_custom_call" | custom-call | tf_op jit(solution)/shard_map/pallas_call | solution.py:344
  21.4 1.4 %shard_map.86 = (bf16[128,2048]{1,0:T(8,128)(2,1)}, bf16[224,2048]{1,0:T(8,128)(2,1)}, bf16[224,2048]{1,0:T(8,128)(2,1)}) custom-call(bf16[128,2048]{1,0:T(8,128)(2,1)S(1)} %get-tuple-element.5.tok_grad, bf16[2,224,2048]{2,1,0:T(8,128)(2,1)S(1)} %get-tuple-element.6.grads), custom_call_target="tpu_custom_call" | custom-call | tf_op jit(solution)/shard_map/pallas_call | solution.py:384
